TPU v7x, 16 devices: a whole 2x2x2 slice. The times are simulated.
16 devices in a mesh: tp: 4 (over z, y), cp: 4 (over x, core).
Axes of the slice: x: 2, y: 2, z: 2, core: 2. Of those that a mesh axis runs over, the one named last changes fastest.
Arguments:
- query_in: bfloat16 [32, 32, 48, 128], P(None, 'cp', 'tp'), parts along dimension 2
- attn_out: bfloat16 [32, 32, 48, 128], P(None, 'cp', 'tp'), parts along dimension 2
- grad_out: bfloat16 [32, 32, 48, 128], P(None, 'cp', 'tp'), parts along dimension 2
- log_sum: float32 [32, 32, 48], P(None, 'cp', 'tp'), parts along dimension 2
- key_cache: bfloat16 [9216, 8, 128], P('cp', 'tp'), parts along dimension 1
- value_cache: bfloat16 [9216, 8, 128], P('cp', 'tp'), parts along dimension 1
Outputs:
- output 1: bfloat16 [32, 32, 48, 128], P(None, 'cp', 'tp'), parts along dimension 2
- output 2: float32 [9216, 8, 128], P('cp', 'tp'), parts along dimension 1
- output 3: float32 [9216, 8, 128], P('cp', 'tp'), parts along dimension 1
There are 4 independent parts. A program takes and returns all parts, laid end to end along the dimension named above; each array names one.
All inputs are finite; a program needn't handle non-finite values.
Results may differ from a plain program's by a relative error of at most 0.001.
Values are sent between devices in bfloat16 or wider.
A program may use at most 1 GiB of HBM per device.

v0:
```python
import jax
import jax.numpy as jnp
from jax import lax
from jax.sharding import PartitionSpec as P


def solution(mesh):
    cp_size = mesh.shape['cp']
    row_spec = P(None, 'cp', 'tp', None)
    lse_spec = P(None, 'cp', 'tp')
    kv_spec = P('cp', 'tp', None)

    def local_backward(query_in, attn_out, grad_out, log_sum, key_cache, value_cache):
        n_slices, local_rows, q_heads, head_dim = query_in.shape
        key_rows = key_cache.shape[0]
        kv_heads = key_cache.shape[1]
        group_size = q_heads // kv_heads
        slice_len = local_rows * cp_size
        prefix = key_rows * cp_size - n_slices * slice_len
        softmax_scale = head_dim ** -0.5
        key_pos = lax.axis_index('cp') * key_rows + jnp.arange(key_rows)
        row_delta = jnp.einsum('sqhd,sqhd->sqh', grad_out, attn_out, preferred_element_type=jnp.float32)

        def slice_step(acc_pair, per_slice):
            grad_key, grad_value = acc_pair
            q_local, g_local, l_local, d_local, slice_idx = per_slice
            q_full = lax.all_gather(q_local, 'cp', axis=0, tiled=True).reshape(slice_len, kv_heads, group_size, head_dim)
            g_full = lax.all_gather(g_local, 'cp', axis=0, tiled=True).reshape(slice_len, kv_heads, group_size, head_dim)
            l_full = lax.all_gather(l_local, 'cp', axis=0, tiled=True).reshape(slice_len, kv_heads, group_size)
            d_full = lax.all_gather(d_local, 'cp', axis=0, tiled=True).reshape(slice_len, kv_heads, group_size)
            row_lse = jnp.transpose(l_full, (1, 2, 0))[..., None]
            row_del = jnp.transpose(d_full, (1, 2, 0))[..., None]
            q_pos = prefix + slice_idx * slice_len + jnp.arange(slice_len)
            causal = key_pos[None, :] <= q_pos[:, None]
            logits = jnp.einsum('qhgd,khd->hgqk', q_full, key_cache, preferred_element_type=jnp.float32)
            prob_f = jnp.where(causal, jnp.exp(logits * softmax_scale - row_lse), 0.0)
            prob_b = prob_f.astype(jnp.bfloat16)
            grad_value = grad_value + jnp.einsum('hgqk,qhgd->khd', prob_b, g_full, preferred_element_type=jnp.float32)
            grad_prob = jnp.einsum('qhgd,khd->hgqk', g_full, value_cache, preferred_element_type=jnp.float32)
            grad_score = (prob_f * (grad_prob - row_del)).astype(jnp.bfloat16)
            grad_key = grad_key + softmax_scale * jnp.einsum('hgqk,qhgd->khd', grad_score, q_full, preferred_element_type=jnp.float32)
            part_q = jnp.einsum('hgqk,khd->qhgd', grad_score, key_cache, preferred_element_type=jnp.float32)
            summed_q = lax.psum_scatter(part_q.reshape(slice_len, q_heads, head_dim), 'cp', scatter_dimension=0, tiled=True)
            return (grad_key, grad_value), (summed_q * softmax_scale).astype(jnp.bfloat16)

        zero_acc = jnp.zeros((key_rows, kv_heads, head_dim), jnp.float32)
        (grad_key, grad_value), grad_query = lax.scan(slice_step, (zero_acc, zero_acc), (query_in, grad_out, log_sum, row_delta, jnp.arange(n_slices)), reverse=True)
        return grad_query, grad_key, grad_value

    return jax.shard_map(local_backward, mesh=mesh, in_specs=(row_spec, row_spec, row_spec, lse_spec, kv_spec, kv_spec), out_specs=(row_spec, kv_spec, kv_spec), check_vma=False)
```

profile of v0, /device:TPU:0, one launch (start us, length us, event | category | flops | bytes accessed | tf_op | source)
XLA Modules:
  0.0 1536.8 jit_solution(2330505895406786837)
XLA Ops:
  14.0 1508.1 %while.19 = (s32[]{:T(128)}, f32[2304,2,128]{0,2,1:T(8,128)}, f32[2304,2,128]{0,2,1:T(8,128)}, bf16[32,8,12,128]{3,1,2,0:T(8,128)(2,1)}, bf16[32,8,12,128]{3,1,2...) while((s32[]{:T(128)}, f32[2304,2,128]{0,2,1:T(8,128)}, ...), condition=%wide.region_2.3_spmd.clone, body=%wide.region_0.2_spmd.clone.sunk | while | flops 1141704960 | bytes 49707860 | solution.py:47
  16.7 6.4 all-gather.13
  23.2 5.4 all-gather.15
  30.2 5.4 all-gather.12
  35.5 5.4 all-gather.14
  50.9 11.5 reduce-scatter.2.cloned.1.call-done
  78.5 5.4 all-gather.12
  83.9 5.4 all-gather.14
  101.7 7.9 reduce-scatter.2.cloned.1.call-done
  125.6 5.4 all-gather.12
  130.9 5.4 all-gather.14
  148.7 7.8 reduce-scatter.2.cloned.1.call-done
  172.6 5.4 all-gather.12
  178.0 5.4 all-gather.14
  195.8 7.8 reduce-scatter.2.cloned.1.call-done
  219.7 5.4 all-gather.12
  225.0 5.4 all-gather.14
  242.8 7.8 reduce-scatter.2.cloned.1.call-done
  266.7 5.4 all-gather.12
  272.1 5.4 all-gather.14
  289.8 7.8 reduce-scatter.2.cloned.1.call-done
  313.7 5.4 all-gather.12
  336.9 7.8 reduce-scatter.2.cloned.1.call-done
  383.9 7.8 reduce-scatter.2.cloned.1.call-done
  431.0 7.8 reduce-scatter.2.cloned.1.call-done
  478.0 7.8 reduce-scatter.2.cloned.1.call-done
  525.0 7.8 reduce-scatter.2.cloned.1.call-done
  572.1 7.8 reduce-scatter.2.cloned.1.call-done
  619.1 7.8 reduce-scatter.2.cloned.1.call-done
  666.2 7.8 reduce-scatter.2.cloned.1.call-done
  713.2 7.8 reduce-scatter.2.cloned.1.call-done
  760.2 7.8 reduce-scatter.2.cloned.1.call-done
  807.3 7.8 reduce-scatter.2.cloned.1.call-done
  854.3 7.8 reduce-scatter.2.cloned.1.call-done
  901.4 7.8 reduce-scatter.2.cloned.1.call-done
  948.4 7.8 reduce-scatter.2.cloned.1.call-done
  995.4 7.8 reduce-scatter.2.cloned.1.call-done
  1042.5 7.8 reduce-scatter.2.cloned.1.call-done
  1089.5 7.8 reduce-scatter.2.cloned.1.call-done
  1136.6 7.8 reduce-scatter.2.cloned.1.call-done
  1183.6 7.8 reduce-scatter.2.cloned.1.call-done
  1230.6 7.8 reduce-scatter.2.cloned.1.call-done
  1277.7 7.8 reduce-scatter.2.cloned.1.call-done
  1324.7 7.8 reduce-scatter.2.cloned.1.call-done
  1371.8 7.8 reduce-scatter.2.cloned.1.call-done
  1418.8 7.8 reduce-scatter.2.cloned.1.call-done
  1465.8 7.8 reduce-scatter.2.cloned.1.call-done
  1512.9 7.8 reduce-scatter.2.cloned.1.call-done
  (898 shorter events, 1166.9 us)
Async XLA Ops:
  7.2 4.5 copy-start.3
  7.2 4.7 copy-start.4
  14.0 48.4 %reduce-scatter.2.cloned.1.call-start = ((), (), s32[]{:S(2)}) async-start(), calls=%async_computation.1 | async-start | bytes 245760 | tf_op jit(solution)/shard_map/while/body/eval_jaxpr/reduce_scatter | solution.py:43
  42.0 1.7 copy-start
  63.9 45.7 %reduce-scatter.2.cloned.1.call-start = ((), (), s32[]{:S(2)}) async-start(), calls=%async_computation.1 | async-start | bytes 245760 | tf_op jit(solution)/shard_map/while/body/eval_jaxpr/reduce_scatter | solution.py:43
  90.3 1.7 copy-start
  110.9 45.6 %reduce-scatter.2.cloned.1.call-start = ((), (), s32[]{:S(2)}) async-start(), calls=%async_computation.1 | async-start | bytes 245760 | tf_op jit(solution)/shard_map/while/body/eval_jaxpr/reduce_scatter | solution.py:43
  137.4 1.7 copy-start
  158.0 45.6 %reduce-scatter.2.cloned.1.call-start = ((), (), s32[]{:S(2)}) async-start(), calls=%async_computation.1 | async-start | bytes 245760 | tf_op jit(solution)/shard_map/while/body/eval_jaxpr/reduce_scatter | solution.py:43
  184.4 1.7 copy-start
  205.0 45.6 %reduce-scatter.2.cloned.1.call-start = ((), (), s32[]{:S(2)}) async-start(), calls=%async_computation.1 | async-start | bytes 245760 | tf_op jit(solution)/shard_map/while/body/eval_jaxpr/reduce_scatter | solution.py:43
  231.4 1.7 copy-start
  252.1 45.6 %reduce-scatter.2.cloned.1.call-start = ((), (), s32[]{:S(2)}) async-start(), calls=%async_computation.1 | async-start | bytes 245760 | tf_op jit(solution)/shard_map/while/body/eval_jaxpr/reduce_scatter | solution.py:43
  278.5 1.7 copy-start
  299.1 45.6 %reduce-scatter.2.cloned.1.call-start = ((), (), s32[]{:S(2)}) async-start(), calls=%async_computation.1 | async-start | bytes 245760 | tf_op jit(solution)/shard_map/while/body/eval_jaxpr/reduce_scatter | solution.py:43
  325.5 1.7 copy-start
  346.1 45.6 %reduce-scatter.2.cloned.1.call-start = ((), (), s32[]{:S(2)}) async-start(), calls=%async_computation.1 | async-start | bytes 245760 | tf_op jit(solution)/shard_map/while/body/eval_jaxpr/reduce_scatter | solution.py:43
  372.5 1.7 copy-start
  393.2 45.6 %reduce-scatter.2.cloned.1.call-start = ((), (), s32[]{:S(2)}) async-start(), calls=%async_computation.1 | async-start | bytes 245760 | tf_op jit(solution)/shard_map/while/body/eval_jaxpr/reduce_scatter | solution.py:43
  419.6 1.7 copy-start
  440.2 45.6 %reduce-scatter.2.cloned.1.call-start = ((), (), s32[]{:S(2)}) async-start(), calls=%async_computation.1 | async-start | bytes 245760 | tf_op jit(solution)/shard_map/while/body/eval_jaxpr/reduce_scatter | solution.py:43
  466.6 1.7 copy-start
  487.3 45.6 %reduce-scatter.2.cloned.1.call-start = ((), (), s32[]{:S(2)}) async-start(), calls=%async_computation.1 | async-start | bytes 245760 | tf_op jit(solution)/shard_map/while/body/eval_jaxpr/reduce_scatter | solution.py:43
  513.7 1.7 copy-start
  534.3 45.6 %reduce-scatter.2.cloned.1.call-start = ((), (), s32[]{:S(2)}) async-start(), calls=%async_computation.1 | async-start | bytes 245760 | tf_op jit(solution)/shard_map/while/body/eval_jaxpr/reduce_scatter | solution.py:43
  560.7 1.7 copy-start
  581.3 45.6 %reduce-scatter.2.cloned.1.call-start = ((), (), s32[]{:S(2)}) async-start(), calls=%async_computation.1 | async-start | bytes 245760 | tf_op jit(solution)/shard_map/while/body/eval_jaxpr/reduce_scatter | solution.py:43
  607.7 1.7 copy-start
  628.4 45.6 %reduce-scatter.2.cloned.1.call-start = ((), (), s32[]{:S(2)}) async-start(), calls=%async_computation.1 | async-start | bytes 245760 | tf_op jit(solution)/shard_map/while/body/eval_jaxpr/reduce_scatter | solution.py:43
  675.4 45.6 %reduce-scatter.2.cloned.1.call-start = ((), (), s32[]{:S(2)}) async-start(), calls=%async_computation.1 | async-start | bytes 245760 | tf_op jit(solution)/shard_map/while/body/eval_jaxpr/reduce_scatter | solution.py:43
  722.5 45.6 %reduce-scatter.2.cloned.1.call-start = ((), (), s32[]{:S(2)}) async-start(), calls=%async_computation.1 | async-start | bytes 245760 | tf_op jit(solution)/shard_map/while/body/eval_jaxpr/reduce_scatter | solution.py:43
  769.5 45.6 %reduce-scatter.2.cloned.1.call-start = ((), (), s32[]{:S(2)}) async-start(), calls=%async_computation.1 | async-start | bytes 245760 | tf_op jit(solution)/shard_map/while/body/eval_jaxpr/reduce_scatter | solution.py:43
  816.5 45.6 %reduce-scatter.2.cloned.1.call-start = ((), (), s32[]{:S(2)}) async-start(), calls=%async_computation.1 | async-start | bytes 245760 | tf_op jit(solution)/shard_map/while/body/eval_jaxpr/reduce_scatter | solution.py:43
  863.6 45.6 %reduce-scatter.2.cloned.1.call-start = ((), (), s32[]{:S(2)}) async-start(), calls=%async_computation.1 | async-start | bytes 245760 | tf_op jit(solution)/shard_map/while/body/eval_jaxpr/reduce_scatter | solution.py:43
  910.6 45.6 %reduce-scatter.2.cloned.1.call-start = ((), (), s32[]{:S(2)}) async-start(), calls=%async_computation.1 | async-start | bytes 245760 | tf_op jit(solution)/shard_map/while/body/eval_jaxpr/reduce_scatter | solution.py:43
  957.7 45.6 %reduce-scatter.2.cloned.1.call-start = ((), (), s32[]{:S(2)}) async-start(), calls=%async_computation.1 | async-start | bytes 245760 | tf_op jit(solution)/shard_map/while/body/eval_jaxpr/reduce_scatter | solution.py:43
  1004.7 45.6 %reduce-scatter.2.cloned.1.call-start = ((), (), s32[]{:S(2)}) async-start(), calls=%async_computation.1 | async-start | bytes 245760 | tf_op jit(solution)/shard_map/while/body/eval_jaxpr/reduce_scatter | solution.py:43
  1051.7 45.6 %reduce-scatter.2.cloned.1.call-start = ((), (), s32[]{:S(2)}) async-start(), calls=%async_computation.1 | async-start | bytes 245760 | tf_op jit(solution)/shard_map/while/body/eval_jaxpr/reduce_scatter | solution.py:43
  1098.8 45.6 %reduce-scatter.2.cloned.1.call-start = ((), (), s32[]{:S(2)}) async-start(), calls=%async_computation.1 | async-start | bytes 245760 | tf_op jit(solution)/shard_map/while/body/eval_jaxpr/reduce_scatter | solution.py:43
  1145.8 45.6 %reduce-scatter.2.cloned.1.call-start = ((), (), s32[]{:S(2)}) async-start(), calls=%async_computation.1 | async-start | bytes 245760 | tf_op jit(solution)/shard_map/while/body/eval_jaxpr/reduce_scatter | solution.py:43
  1192.9 45.6 %reduce-scatter.2.cloned.1.call-start = ((), (), s32[]{:S(2)}) async-start(), calls=%async_computation.1 | async-start | bytes 245760 | tf_op jit(solution)/shard_map/while/body/eval_jaxpr/reduce_scatter | solution.py:43
  1239.9 45.6 %reduce-scatter.2.cloned.1.call-start = ((), (), s32[]{:S(2)}) async-start(), calls=%async_computation.1 | async-start | bytes 245760 | tf_op jit(solution)/shard_map/while/body/eval_jaxpr/reduce_scatter | solution.py:43
  1286.9 45.6 %reduce-scatter.2.cloned.1.call-start = ((), (), s32[]{:S(2)}) async-start(), calls=%async_computation.1 | async-start | bytes 245760 | tf_op jit(solution)/shard_map/while/body/eval_jaxpr/reduce_scatter | solution.py:43
  1334.0 45.6 %reduce-scatter.2.cloned.1.call-start = ((), (), s32[]{:S(2)}) async-start(), calls=%async_computation.1 | async-start | bytes 245760 | tf_op jit(solution)/shard_map/while/body/eval_jaxpr/reduce_scatter | solution.py:43
  1381.0 45.6 %reduce-scatter.2.cloned.1.call-start = ((), (), s32[]{:S(2)}) async-start(), calls=%async_computation.1 | async-start | bytes 245760 | tf_op jit(solution)/shard_map/while/body/eval_jaxpr/reduce_scatter | solution.py:43
  1428.1 45.6 %reduce-scatter.2.cloned.1.call-start = ((), (), s32[]{:S(2)}) async-start(), calls=%async_computation.1 | async-start | bytes 245760 | tf_op jit(solution)/shard_map/while/body/eval_jaxpr/reduce_scatter | solution.py:43
  1475.1 45.6 %reduce-scatter.2.cloned.1.call-start = ((), (), s32[]{:S(2)}) async-start(), calls=%async_computation.1 | async-start | bytes 245760 | tf_op jit(solution)/shard_map/while/body/eval_jaxpr/reduce_scatter | solution.py:43
  1522.1 5.1 copy-start.1
  (51 other events, 74.0 us)
Sparse Core Ops, SparseCore 0:
  45.1 17.2 reduce-scatter.1
  93.5 16.0 reduce-scatter.1
  140.5 15.9 reduce-scatter.1
  187.6 15.9 reduce-scatter.1
  234.6 15.9 reduce-scatter.1
  281.7 15.9 reduce-scatter.1
  328.7 15.9 reduce-scatter.1
  375.7 15.9 reduce-scatter.1
  422.8 15.9 reduce-scatter.1
  469.8 15.9 reduce-scatter.1
  516.9 15.9 reduce-scatter.1
  563.9 15.9 reduce-scatter.1
  610.9 15.9 reduce-scatter.1
  658.0 15.9 reduce-scatter.1
  705.0 15.9 reduce-scatter.1
  752.1 15.9 reduce-scatter.1
  799.1 15.9 reduce-scatter.1
  846.1 15.9 reduce-scatter.1
  893.2 15.9 reduce-scatter.1
  940.2 15.9 reduce-scatter.1
  987.3 15.9 reduce-scatter.1
  1034.3 15.9 reduce-scatter.1
  1081.3 15.9 reduce-scatter.1
  1128.4 15.9 reduce-scatter.1
  1175.4 15.9 reduce-scatter.1
  1222.5 15.9 reduce-scatter.1
  1269.5 15.9 reduce-scatter.1
  1316.5 15.9 reduce-scatter.1
  1363.6 15.9 reduce-scatter.1
  1410.6 15.9 reduce-scatter.1
  1457.7 15.9 reduce-scatter.1
  1504.7 15.9 reduce-scatter.1
where the time goes:
time: 1550 us; the launch traced here: 1540 us
  blocking collectives  675 us (44%)
  matrix products  354 us (23%)
  waiting for transfers between devices  255 us (16%)
  local copies, waits for them, and re-layouts  168 us (11%)
  other arithmetic  50.8 us (3%)
  loops' own time  19.9 us (1%)
    reduce_scatter x32, waiting for transfers between devices, slice_step(): lax.psum_scatter(part_q.reshape(slice_len, q_heads, head_dim), 'cp', scat...  255 us
    all_gather x32, blocking collectives, slice_step(): lax.all_gather(g_local, 'cp', axis=0, tiled=True)  172 us
    all_gather x32, blocking collectives, slice_step(): lax.all_gather(q_local, 'cp', axis=0, tiled=True)  172 us
    all_gather x32, blocking collectives, slice_step(): lax.all_gather(l_local, 'cp', axis=0, tiled=True)  166 us
    all_gather x32, blocking collectives, slice_step(): lax.all_gather(d_local, 'cp', axis=0, tiled=True)  165 us
    dot_general x32, matrix products, slice_step(): jnp.einsum('hgqk,qhgd->khd', prob_b, g_full, preferred_element_type=jnp.f...  149 us
    dynamic_slice x160, local copies, waits for them, and re-layouts, local_backward(): lax.scan(slice_step, (zero_acc, zero_acc), (query_in, grad_out, log_sum,...  114 us
    dot_general x32, matrix products, slice_step(): jnp.einsum('hgqk,qhgd->khd', grad_score, q_full, preferred_element_type=j...  114 us
  transfers between devices with their start and end apart: 32, of which 32 were waited for; matrix products, arithmetic and copies ran while one was open for 17% of the time, Pallas kernels for 0%

commit v1 on v0

v1 whole, which is shorter than its diff:
```python
import jax
import jax.numpy as jnp
from jax import lax
from jax.experimental import pallas as pl
from jax.experimental.pallas import tpu as pltpu
from jax.sharding import PartitionSpec as P

MESH = pl.DeviceIdType.MESH
LOG2E = 1.4426950408889634
NT = (((1,), (1,)), ((), ()))
NN = (((1,), (0,)), ((), ()))
KEY_BLOCK = 256
OWN, PEER, ACROSS, DIAG = 0, 1, 2, 3
STEPS = [(0, 0), (1, 0), (0, 1), (2, 0), (3, 0), (1, 1), (2, 1), (3, 1), (0, 2), (2, 2), (3, 2), (1, 2), (2, 3), (3, 3), (0, 3), (1, 3)]
REDUCE_AT = [5, 8, 11, 14]


def dot(a, b, dims=NN):
    return lax.dot_general(a, b, dims, preferred_element_type=jnp.float32)


def table(step, values):
    out = jnp.int32(values[0])
    for i, v in enumerate(values[1:], 1):
        out = jnp.where(step == i, jnp.int32(v), out)
    return out


def make_kernel(n_slices, rows8, group, head_dim, key_rows, cp_size):
    half_slices = n_slices // 2
    unit = rows8 * group
    rows = half_slices * unit
    slice_len = rows8 * cp_size
    prefix = key_rows * cp_size - n_slices * slice_len
    n_blocks = key_rows // KEY_BLOCK
    scale = head_dim ** -0.5
    exp_scale = scale * LOG2E
    first_masked = max(0, prefix - (cp_size - 1) * key_rows) // KEY_BLOCK

    def kernel(q_hbm, o_hbm, g_hbm, l_hbm, k_hbm, v_hbm, dq_hbm, dk_hbm, dv_hbm,
               q_all, g_all, stat_all, o_own, lse_own, k_all, v_all, dk_t, dv_t, dq_all,
               from_peer_own, from_peer_across, from_across, q_t, g_t, p_a, s_a, p_b, s_b,
               lse_rep, del_rep, row_pos, dq_out, dk_out, dv_out,
               load_sem, q_recv, g_recv, stat_recv, q_send, g_send, stat_send,
               part_recv, part_send, store_sem):
        me = lax.axis_index('cp')
        chip, core = me // 2, me % 2
        peer = chip * 2 + (1 - core)
        across = (1 - chip) * 2 + core
        diag = (1 - chip) * 2 + (1 - core)

        barrier = pltpu.get_barrier_semaphore()
        for other in (peer, across):
            pl.semaphore_signal(barrier, inc=1, device_id={'cp': other}, device_id_type=MESH)

        def part(ref, ch):
            return ref.at[pl.ds((ch % 2) * half_slices, half_slices), ch // 2]

        loads = []
        for ch in range(4):
            loads.append(pltpu.make_async_copy(part(g_hbm, ch), g_all.at[OWN, ch], load_sem.at[ch]))
        for ch in range(4):
            loads.append(pltpu.make_async_copy(part(o_hbm, ch), o_own.at[ch], load_sem.at[4 + ch]))
        loads.append(pltpu.make_async_copy(l_hbm, lse_own, load_sem.at[8]))
        for ch in range(4):
            loads.append(pltpu.make_async_copy(part(q_hbm, ch), q_all.at[OWN, ch], load_sem.at[9 + ch]))
        loads.append(pltpu.make_async_copy(k_hbm, k_all, load_sem.at[13]))
        loads.append(pltpu.make_async_copy(v_hbm, v_all, load_sem.at[14]))
        for copy in loads:
            copy.start()

        def send_rows(ch, slot, other):
            q = pltpu.make_async_remote_copy(part(q_hbm, ch), q_all.at[slot, ch], q_send.at[slot, ch], q_recv.at[slot, ch], device_id={'cp': other}, device_id_type=MESH)
            g = pltpu.make_async_remote_copy(part(g_hbm, ch), g_all.at[slot, ch], g_send.at[slot, ch], g_recv.at[slot, ch], device_id={'cp': other}, device_id_type=MESH)
            return q, g

        def send_stat(src_slot, dst_slot, other):
            return pltpu.make_async_remote_copy(stat_all.at[src_slot], stat_all.at[dst_slot], stat_send.at[dst_slot], stat_recv.at[dst_slot], device_id={'cp': other}, device_id_type=MESH)

        def forward_rows(ch):
            q = pltpu.make_async_remote_copy(q_all.at[ACROSS, ch], q_all.at[DIAG, ch], q_send.at[DIAG, ch], q_recv.at[DIAG, ch], device_id={'cp': peer}, device_id_type=MESH)
            g = pltpu.make_async_remote_copy(g_all.at[ACROSS, ch], g_all.at[DIAG, ch], g_send.at[DIAG, ch], g_recv.at[DIAG, ch], device_id={'cp': peer}, device_id_type=MESH)
            return q, g

        def send_own_part(ch):
            return pltpu.make_async_remote_copy(dq_all.at[PEER, ch], from_peer_own.at[ch], part_send.at[0, ch], part_recv.at[0, ch], device_id={'cp': peer}, device_id_type=MESH)

        def send_diag_part(ch):
            return pltpu.make_async_remote_copy(dq_all.at[DIAG, ch], from_peer_across.at[ch], part_send.at[1, ch], part_recv.at[1, ch], device_id={'cp': peer}, device_id_type=MESH)

        def send_reduced(ch):
            return pltpu.make_async_remote_copy(dq_all.at[ACROSS, ch], from_across.at[ch], part_send.at[2, ch], part_recv.at[2, ch], device_id={'cp': across}, device_id_type=MESH)

        pl.semaphore_wait(barrier, 2)
        for slot, other in ((ACROSS, across), (PEER, peer)):
            for copy in send_rows(0, slot, other):
                copy.start()

        for copy in loads[:9]:
            copy.wait()
        lane = lax.broadcasted_iota(jnp.int32, (unit, 128), 1)
        for kv in range(2):
            acc = jnp.zeros((unit, 128), jnp.float32)
            for s in range(n_slices):
                ch = kv * 2 + s // half_slices
                prod = g_all[OWN, ch, s % half_slices].astype(jnp.float32) * o_own[ch, s % half_slices].astype(jnp.float32)
                acc = jnp.where(lane == n_slices + s, jnp.sum(prod, axis=1, keepdims=True), acc)
            stat_all[OWN, pl.ds(kv * group, group)] = acc.reshape(group, rows8, 128)
        stat_all[OWN, :, :, pl.ds(0, n_slices)] = lse_own[...] * LOG2E
        for slot, other in ((ACROSS, across), (PEER, peer)):
            send_stat(OWN, slot, other).start()
        for ch in range(1, 4):
            for slot, other in ((ACROSS, across), (PEER, peer)):
                for copy in send_rows(ch, slot, other):
                    copy.start()

        dk_t[...] = jnp.zeros_like(dk_t)
        dv_t[...] = jnp.zeros_like(dv_t)
        token = lax.broadcasted_iota(jnp.int32, (rows8, 128), 0)
        for s in range(half_slices):
            for h in range(group):
                row_pos[pl.ds((s * group + h) * rows8, rows8)] = token + s * slice_len
        for copy in loads[9:]:
            copy.wait()

        def step_body(step, carry):
            slot = table(step, [a for a, _ in STEPS])
            ch = table(step, [b for _, b in STEPS])
            kv, half = ch // 2, ch % 2
            source = jnp.where(slot == OWN, me, jnp.where(slot == PEER, peer, jnp.where(slot == ACROSS, across, diag)))

            @pl.when(slot != OWN)
            def _():
                pltpu.make_async_remote_copy(q_all.at[slot, ch], q_all.at[slot, ch], q_send.at[slot, ch], q_recv.at[slot, ch], device_id={'cp': peer}, device_id_type=MESH).wait_recv()
                pltpu.make_async_remote_copy(g_all.at[slot, ch], g_all.at[slot, ch], g_send.at[slot, ch], g_recv.at[slot, ch], device_id={'cp': peer}, device_id_type=MESH).wait_recv()

            @pl.when(jnp.logical_and(slot != OWN, ch == 0))
            def _():
                pltpu.make_async_remote_copy(stat_all.at[slot], stat_all.at[slot], stat_send.at[slot], stat_recv.at[slot], device_id={'cp': peer}, device_id_type=MESH).wait_recv()

            @pl.when(slot == ACROSS)
            def _():
                for copy in forward_rows(ch):
                    copy.start()

            @pl.when(jnp.logical_and(slot == ACROSS, ch == 0))
            def _():
                send_stat(ACROSS, DIAG, peer).start()

            q_t[...] = q_all[slot, ch].reshape(rows, head_dim).T
            g_t[...] = g_all[slot, ch].reshape(rows, head_dim).T
            for h in range(group):
                st = stat_all[slot, kv * group + h]
                st = jnp.where(half == 1, pltpu.roll(st, 128 - half_slices, 1), st)
                for s in range(half_slices):
                    at = pl.ds((s * group + h) * rows8, rows8)
                    lse_rep[at] = jnp.broadcast_to(st[:, s:s + 1], (rows8, 128))
                    del_rep[at] = jnp.broadcast_to(st[:, n_slices + s:n_slices + s + 1], (rows8, 128))

            def scores(block, p_buf, s_buf):
                keys = pl.ds(block * KEY_BLOCK, KEY_BLOCK)
                logits = dot(q_all[slot, ch].reshape(rows, head_dim), k_all[kv, keys], NT)
                lse = lse_rep[...]
                prob = jnp.exp2(logits * exp_scale - jnp.concatenate([lse, lse], 1))
                if block >= first_masked:
                    first = me * key_rows + block * KEY_BLOCK - prefix - half * (half_slices * slice_len) - source * rows8
                    key_pos = lax.broadcasted_iota(jnp.int32, (rows, KEY_BLOCK), 1) + first
                    pos = row_pos[...]
                    prob = jnp.where(key_pos <= jnp.concatenate([pos, pos], 1), prob, 0.0)
                grad_prob = dot(g_all[slot, ch].reshape(rows, head_dim), v_all[kv, keys], NT)
                delta = del_rep[...]
                p_buf[...] = prob.astype(jnp.bfloat16)
                s_buf[...] = (prob * (grad_prob - jnp.concatenate([delta, delta], 1))).astype(jnp.bfloat16)

            def grads(block, p_buf, s_buf):
                keys = pl.ds(block * KEY_BLOCK, KEY_BLOCK)
                dv_t[kv, :, keys] += dot(g_t[...], p_buf[...])
                dk_t[kv, :, keys] += dot(q_t[...], s_buf[...])
                part_q = dot(s_buf[...], k_all[kv, keys])
                if block == 0:
                    dq_all[slot, ch] = part_q
                else:
                    dq_all[slot, ch] += part_q

            bufs = ((p_a, s_a), (p_b, s_b))
            scores(0, *bufs[0])
            for block in range(n_blocks):
                if block + 1 < n_blocks:
                    scores(block + 1, *bufs[(block + 1) % 2])
                grads(block, *bufs[block % 2])

            @pl.when(slot == PEER)
            def _():
                send_own_part(ch).start()

            @pl.when(slot == DIAG)
            def _():
                send_diag_part(ch).start()

            reduce_ch = table(step, [REDUCE_AT.index(i) if i in REDUCE_AT else -1 for i in range(len(STEPS))])

            @pl.when(reduce_ch >= 0)
            def _():
                send_diag_part(reduce_ch).wait_recv()
                dq_all[ACROSS, reduce_ch] += from_peer_across[reduce_ch]
                send_reduced(reduce_ch).start()

            return carry

        lax.fori_loop(0, len(STEPS), step_body, 0)

        stores = []
        for i, (acc_t, out, hbm) in enumerate(((dv_t, dv_out, dv_hbm), (dk_t, dk_out, dk_hbm))):
            for block in range(n_blocks):
                keys = pl.ds(block * KEY_BLOCK, KEY_BLOCK)
                for kv in range(2):
                    grad = acc_t[kv, :, keys].T
                    if acc_t is dk_t:
                        grad = grad * scale
                    out[pl.ds(2 * block * KEY_BLOCK + kv, KEY_BLOCK, stride=2)] = grad
            stores.append(pltpu.make_async_copy(out, hbm, store_sem.at[i]))
            stores[-1].start()
        for ch in range(4):
            send_own_part(ch).wait_recv()
            send_reduced(ch).wait_recv()
            total = (dq_all[OWN, ch] + from_peer_own[ch] + from_across[ch]) * scale
            dq_out[ch] = total.astype(jnp.bfloat16).reshape(half_slices, unit, head_dim)
            stores.append(pltpu.make_async_copy(dq_out.at[ch], part(dq_hbm, ch), store_sem.at[2 + ch]))
            stores[-1].start()
        for copy in stores:
            copy.wait()
        for slot, other in ((ACROSS, across), (PEER, peer)):
            send_stat(OWN, slot, other).wait_send()
            for ch in range(4):
                for copy in send_rows(ch, slot, other):
                    copy.wait_send()
        send_stat(ACROSS, DIAG, peer).wait_send()
        for ch in range(4):
            for copy in forward_rows(ch):
                copy.wait_send()
            send_own_part(ch).wait_send()
            send_diag_part(ch).wait_send()
            send_reduced(ch).wait_send()

    bf16, f32 = jnp.bfloat16, jnp.float32
    chunk = (half_slices, unit, head_dim)
    scratch = [
        pltpu.VMEM((4, 4) + chunk, bf16),
        pltpu.VMEM((4, 4) + chunk, bf16),
        pltpu.VMEM((4, 2 * group, rows8, 128), f32),
        pltpu.VMEM((4,) + chunk, bf16),
        pltpu.VMEM((2 * group, rows8, n_slices), f32),
        pltpu.VMEM((2, key_rows, head_dim), bf16),
        pltpu.VMEM((2, key_rows, head_dim), bf16),
        pltpu.VMEM((2, head_dim, key_rows), f32),
        pltpu.VMEM((2, head_dim, key_rows), f32),
        pltpu.VMEM((4, 4, rows, head_dim), f32),
        pltpu.VMEM((4, rows, head_dim), f32),
        pltpu.VMEM((4, rows, head_dim), f32),
        pltpu.VMEM((4, rows, head_dim), f32),
        pltpu.VMEM((head_dim, rows), bf16),
        pltpu.VMEM((head_dim, rows), bf16),
        pltpu.VMEM((rows, KEY_BLOCK), bf16),
        pltpu.VMEM((rows, KEY_BLOCK), bf16),
        pltpu.VMEM((rows, KEY_BLOCK), bf16),
        pltpu.VMEM((rows, KEY_BLOCK), bf16),
        pltpu.VMEM((rows, 128), f32),
        pltpu.VMEM((rows, 128), f32),
        pltpu.VMEM((rows, 128), jnp.int32),
        pltpu.VMEM((4,) + chunk, bf16),
        pltpu.VMEM((2 * key_rows, head_dim), f32),
        pltpu.VMEM((2 * key_rows, head_dim), f32),
        pltpu.SemaphoreType.DMA((15,)),
        pltpu.SemaphoreType.DMA((4, 4)),
        pltpu.SemaphoreType.DMA((4, 4)),
        pltpu.SemaphoreType.DMA((4,)),
        pltpu.SemaphoreType.DMA((4, 4)),
        pltpu.SemaphoreType.DMA((4, 4)),
        pltpu.SemaphoreType.DMA((4,)),
        pltpu.SemaphoreType.DMA((3, 4)),
        pltpu.SemaphoreType.DMA((3, 4)),
        pltpu.SemaphoreType.DMA((6,)),
    ]
    return kernel, scratch


def solution(mesh):
    cp_size = mesh.shape['cp']
    row_spec = P(None, 'cp', 'tp', None)
    lse_spec = P(None, 'cp', 'tp')
    kv_spec = P('cp', 'tp', None)

    def local_backward(query_in, attn_out, grad_out, log_sum, key_cache, value_cache):
        n_slices, rows8, q_heads, head_dim = query_in.shape
        key_rows, kv_heads, _ = key_cache.shape
        group = q_heads // kv_heads
        kernel, scratch = make_kernel(n_slices, rows8, group, head_dim, key_rows, cp_size)

        def by_head(x):
            return x.transpose(0, 2, 1, 3).reshape(n_slices, kv_heads, group * rows8, head_dim)

        hbm = pl.BlockSpec(memory_space=pl.ANY)
        grad_q, grad_k, grad_v = pl.pallas_call(
            kernel,
            out_shape=(
                jax.ShapeDtypeStruct((n_slices, kv_heads, group * rows8, head_dim), jnp.bfloat16),
                jax.ShapeDtypeStruct((key_rows * kv_heads, head_dim), jnp.float32),
                jax.ShapeDtypeStruct((key_rows * kv_heads, head_dim), jnp.float32),
            ),
            in_specs=[hbm] * 6,
            out_specs=(hbm,) * 3,
            scratch_shapes=scratch,
            compiler_params=pltpu.CompilerParams(collective_id=0, has_side_effects=True, vmem_limit_bytes=60 * 2 ** 20),
        )(by_head(query_in), by_head(attn_out), by_head(grad_out), log_sum.transpose(2, 1, 0),
          key_cache.transpose(1, 0, 2), value_cache.transpose(1, 0, 2))
        grad_q = grad_q.reshape(n_slices, q_heads, rows8, head_dim).transpose(0, 2, 1, 3)
        return grad_q, grad_k.reshape(key_rows, kv_heads, head_dim), grad_v.reshape(key_rows, kv_heads, head_dim)

    return jax.shard_map(local_backward, mesh=mesh, in_specs=(row_spec, row_spec, row_spec, lse_spec, kv_spec, kv_spec), out_specs=(row_spec, kv_spec, kv_spec), check_vma=False)
```

time: 1550 us -> 91.3 us (0.06)
  blocking collectives: 675 us -> 0 us
  matrix products: 354 us -> 0 us
  waiting for transfers between devices: 255 us -> 0 us
  local copies, waits for them, and re-layouts: 168 us -> 10.8 us
  Pallas kernels: 0 us -> 79.6 us
  other arithmetic: 50.8 us -> 0 us
  loops' own time: 19.9 us -> 0 us
    all_gather x128 -> x0, blocking collectives: 675 us -> none  [the longest x32 172 us: slice_step(): lax.all_gather(g_local, 'cp', axis=0, tiled=True)]
    dot_general x160 -> x0, matrix products: 354 us -> none  [the longest x32 149 us: slice_step(): jnp.einsum('hgqk,qhgd->khd', prob_b, g_full, preferred_element_type=jnp.f...]
    reduce_scatter x32 -> x0, waiting for transfers between devices: 255 us -> none  [slice_step(): lax.psum_scatter(part_q.reshape(slice_len, q_heads, head_dim), 'cp', scat...]
    dynamic_slice x160 -> x0, local copies, waits for them, and re-layouts: 114 us -> none  [local_backward(): lax.scan(slice_step, (zero_acc, zero_acc), (query_in, grad_out, log_sum,...]
    pallas_call x0 -> x1, Pallas kernels: none -> 79.6 us  [local_backward(): pl.pallas_call(kernel, out_shape=(jax.ShapeDtypeStruct((n_slices, kv_head...]
    dynamic_update_slice x32 -> x0, other arithmetic: 45.2 us -> none  [local_backward(): lax.scan(slice_step, (zero_acc, zero_acc), (query_in, grad_out, log_sum,...]
    while x128 -> x0, local copies, waits for them, and re-layouts: 35.3 us -> none
    another operation x1 -> x0, loops' own time: 19.9 us -> none  [local_backward(): lax.scan(slice_step, (zero_acc, zero_acc), (query_in, grad_out, log_sum,...]
  transfers between devices with their start and end apart: 32 -> 0, of which waited for: 32 -> 0; matrix products, arithmetic and copies ran while one was open for 17% -> 0% of each run, Pallas kernels for 0% -> 0%
where the time goes in v1:
time: 91.3 us; the launch traced here: 91.1 us
  Pallas kernels  79.6 us (87%)
  local copies, waits for them, and re-layouts  10.8 us (12%)
    pallas_call x1, Pallas kernels, local_backward(): pl.pallas_call(kernel, out_shape=(jax.ShapeDtypeStruct((n_slices, kv_head...  79.6 us
    unnamed x5, local copies, waits for them, and re-layouts  7.49 us
    transpose x1, local copies, waits for them, and re-layouts, local_backward(): value_cache.transpose(1, 0, 2)  3.33 us

profile of v1, /device:TPU:0, one launch (start us, length us, event | category | flops | bytes accessed | tf_op | source)
XLA Modules:
  0.0 91.1 jit_solution(1079744946116860330)
XLA Ops:
  0.6 3.3 %copy_bitcast_fusion = (bf16[2,2304,128]{2,1,0:T(8,128)(2,1)}, bf16[2,2304,128]{2,1,0:T(8,128)(2,1)}) fusion(bf16[2304,2,128]{2,1,0:T(2,128)(2,1)} %param.11, bf16[2304,2,128]{2,1,0:T(2,128)(2,1)} %param.10), kind=kLoop, calls=%fused_computation | loop fusion | bytes 4718592 | tf_op jit(solution)/shard_map/transpose | solution.py:315
  4.0 79.6 %shard_map.85 = (bf16[32,2,48,128]{3,2,1,0:T(8,128)(2,1)}, f32[4608,128]{1,0:T(8,128)}, f32[4608,128]{1,0:T(8,128)}) custom-call(bf16[32,2,48,128]{3,2,1,0:T(8,128)(2,1)} %bitcast.21, bf16[32,2,48,128]{3,2,1,0:T(8,128)(2,1)} %bitcast.22, bf16[32,2,48,128]{3,2,1,0:T(8,128)(2,1)} %bitcast.23, f32[12,8,32]{2,1,0:T(8,128)} %bitcast.25, ...), custom_call_target="tpu_custom_call" | custom-call | tf_op jit(solution)/shard_map/pallas_call | solution.py:303
  83.6 2.1 %copy.16 = bf16[32,8,12,128]{3,1,2,0:T(8,128)(2,1)} copy(bf16[32,8,12,128]{3,1,2,0:T(8,128)(2,1)} %bitcast.24) | data formatting | bytes 1572864
  85.6 0.0 copy-start
  85.7 4.0 %copy.17 = f32[2304,2,128]{2,1,0:T(2,128)} copy(f32[2304,2,128]{2,1,0:T(2,128)} %bitcast.20) | data formatting | bytes 4718592
  89.7 0.0 copy-done
  89.7 1.4 %copy.18 = f32[2304,2,128]{2,1,0:T(2,128)} copy(f32[2304,2,128]{2,1,0:T(2,128)S(1)} %bitcast.19) | data formatting | bytes 4718592
Async XLA Ops:
  85.6 4.0 %copy-start = (f32[4608,128]{1,0:T(8,128)S(1)}, f32[4608,128]{1,0:T(8,128)}, u32[]{:S(2)}) copy-start(f32[4608,128]{1,0:T(8,128)} %get-tuple-element.8) | copy-start | bytes 7077892

commit v2 on v1

--- a/solution.py
+++ b/solution.py
@@ -37,12 +37,12 @@
     exp_scale = scale * LOG2E
     first_masked = max(0, prefix - (cp_size - 1) * key_rows) // KEY_BLOCK
 
-    def kernel(q_hbm, o_hbm, g_hbm, l_hbm, k_hbm, v_hbm, dq_hbm, dk_hbm, dv_hbm,
-               q_all, g_all, stat_all, o_own, lse_own, k_all, v_all, dk_t, dv_t, dq_all,
+    def kernel(q_hbm, o_hbm, g_hbm, l_hbm, k_hbm, v_hbm, dq_out, dk_out, dv_out,
+               q_all, g_all, stat_all, o_own, lse_own, k_raw, v_raw, k_all, v_all, dk_t, dv_t, dq_all,
                from_peer_own, from_peer_across, from_across, q_t, g_t, p_a, s_a, p_b, s_b,
-               lse_rep, del_rep, row_pos, dq_out, dk_out, dv_out,
+               lse_rep, del_rep, row_pos,
                load_sem, q_recv, g_recv, stat_recv, q_send, g_send, stat_send,
-               part_recv, part_send, store_sem):
+               part_recv, part_send):
         me = lax.axis_index('cp')
         chip, core = me // 2, me % 2
         peer = chip * 2 + (1 - core)
@@ -64,8 +64,8 @@
         loads.append(pltpu.make_async_copy(l_hbm, lse_own, load_sem.at[8]))
         for ch in range(4):
             loads.append(pltpu.make_async_copy(part(q_hbm, ch), q_all.at[OWN, ch], load_sem.at[9 + ch]))
-        loads.append(pltpu.make_async_copy(k_hbm, k_all, load_sem.at[13]))
-        loads.append(pltpu.make_async_copy(v_hbm, v_all, load_sem.at[14]))
+        loads.append(pltpu.make_async_copy(k_hbm, k_raw, load_sem.at[13]))
+        loads.append(pltpu.make_async_copy(v_hbm, v_raw, load_sem.at[14]))
         for copy in loads:
             copy.start()
 
@@ -122,6 +122,12 @@
                 row_pos[pl.ds((s * group + h) * rows8, rows8)] = token + s * slice_len
         for copy in loads[9:]:
             copy.wait()
+        for raw, wide, split in ((k_raw, dk_out, k_all), (v_raw, dv_out, v_all)):
+            for block in range(n_blocks):
+                both = pl.ds(2 * block * KEY_BLOCK, 2 * KEY_BLOCK)
+                wide[both] = raw[both].astype(jnp.float32)
+                for kv in range(2):
+                    split[kv, pl.ds(block * KEY_BLOCK, KEY_BLOCK)] = wide[pl.ds(2 * block * KEY_BLOCK + kv, KEY_BLOCK, stride=2)].astype(jnp.bfloat16)
 
         def step_body(step, carry):
             slot = table(step, [a for a, _ in STEPS])
@@ -209,26 +215,16 @@
 
         lax.fori_loop(0, len(STEPS), step_body, 0)
 
-        stores = []
-        for i, (acc_t, out, hbm) in enumerate(((dv_t, dv_out, dv_hbm), (dk_t, dk_out, dk_hbm))):
+        for acc_t, out, factor in ((dv_t, dv_out, None), (dk_t, dk_out, scale)):
             for block in range(n_blocks):
-                keys = pl.ds(block * KEY_BLOCK, KEY_BLOCK)
                 for kv in range(2):
-                    grad = acc_t[kv, :, keys].T
-                    if acc_t is dk_t:
-                        grad = grad * scale
-                    out[pl.ds(2 * block * KEY_BLOCK + kv, KEY_BLOCK, stride=2)] = grad
-            stores.append(pltpu.make_async_copy(out, hbm, store_sem.at[i]))
-            stores[-1].start()
+                    grad = acc_t[kv, :, pl.ds(block * KEY_BLOCK, KEY_BLOCK)].T
+                    out[pl.ds(2 * block * KEY_BLOCK + kv, KEY_BLOCK, stride=2)] = grad if factor is None else grad * factor
         for ch in range(4):
             send_own_part(ch).wait_recv()
             send_reduced(ch).wait_recv()
             total = (dq_all[OWN, ch] + from_peer_own[ch] + from_across[ch]) * scale
-            dq_out[ch] = total.astype(jnp.bfloat16).reshape(half_slices, unit, head_dim)
-            stores.append(pltpu.make_async_copy(dq_out.at[ch], part(dq_hbm, ch), store_sem.at[2 + ch]))
-            stores[-1].start()
-        for copy in stores:
-            copy.wait()
+            dq_out[pl.ds((ch % 2) * half_slices, half_slices), ch // 2] = total.astype(jnp.bfloat16).reshape(half_slices, unit, head_dim)
         for slot, other in ((ACROSS, across), (PEER, peer)):
             send_stat(OWN, slot, other).wait_send()
             for ch in range(4):
@@ -250,6 +246,8 @@
         pltpu.VMEM((4, 2 * group, rows8, 128), f32),
         pltpu.VMEM((4,) + chunk, bf16),
         pltpu.VMEM((2 * group, rows8, n_slices), f32),
+        pltpu.VMEM((2 * key_rows, head_dim), bf16),
+        pltpu.VMEM((2 * key_rows, head_dim), bf16),
         pltpu.VMEM((2, key_rows, head_dim), bf16),
         pltpu.VMEM((2, key_rows, head_dim), bf16),
         pltpu.VMEM((2, head_dim, key_rows), f32),
@@ -267,9 +265,6 @@
         pltpu.VMEM((rows, 128), f32),
         pltpu.VMEM((rows, 128), f32),
         pltpu.VMEM((rows, 128), jnp.int32),
-        pltpu.VMEM((4,) + chunk, bf16),
-        pltpu.VMEM((2 * key_rows, head_dim), f32),
-        pltpu.VMEM((2 * key_rows, head_dim), f32),
         pltpu.SemaphoreType.DMA((15,)),
         pltpu.SemaphoreType.DMA((4, 4)),
         pltpu.SemaphoreType.DMA((4, 4)),
@@ -279,9 +274,16 @@
         pltpu.SemaphoreType.DMA((4,)),
         pltpu.SemaphoreType.DMA((3, 4)),
         pltpu.SemaphoreType.DMA((3, 4)),
-        pltpu.SemaphoreType.DMA((6,)),
     ]
     return kernel, scratch
+
+
+def store_results(dq_in, dk_in, dv_in, dq_hbm, dk_hbm, dv_hbm, sem):
+    copies = [pltpu.make_async_copy(a, b, sem.at[i]) for i, (a, b) in enumerate(((dk_in, dk_hbm), (dv_in, dv_hbm), (dq_in, dq_hbm)))]
+    for copy in copies:
+        copy.start()
+    for copy in copies:
+        copy.wait()
 
 
 def solution(mesh):
@@ -299,7 +301,7 @@
         def by_head(x):
             return x.transpose(0, 2, 1, 3).reshape(n_slices, kv_heads, group * rows8, head_dim)
 
-        hbm = pl.BlockSpec(memory_space=pl.ANY)
+        hbm, vmem = pl.BlockSpec(memory_space=pltpu.HBM), pl.BlockSpec(memory_space=pltpu.VMEM)
         grad_q, grad_k, grad_v = pl.pallas_call(
             kernel,
             out_shape=(
@@ -308,11 +310,20 @@
                 jax.ShapeDtypeStruct((key_rows * kv_heads, head_dim), jnp.float32),
             ),
             in_specs=[hbm] * 6,
+            out_specs=(vmem,) * 3,
+            scratch_shapes=scratch,
+            compiler_params=pltpu.CompilerParams(collective_id=0, has_side_effects=True, vmem_limit_bytes=40 * 2 ** 20),
+        )(*(pltpu.with_memory_space_constraint(x, pltpu.HBM) for x in (
+            by_head(query_in), by_head(attn_out), by_head(grad_out), log_sum.transpose(2, 1, 0),
+            key_cache.reshape(key_rows * kv_heads, head_dim), value_cache.reshape(key_rows * kv_heads, head_dim))))
+        grad_q, grad_k, grad_v = pl.pallas_call(
+            store_results,
+            out_shape=tuple(jax.ShapeDtypeStruct(x.shape, x.dtype) for x in (grad_q, grad_k, grad_v)),
+            in_specs=[vmem] * 3,
             out_specs=(hbm,) * 3,
-            scratch_shapes=scratch,
-            compiler_params=pltpu.CompilerParams(collective_id=0, has_side_effects=True, vmem_limit_bytes=60 * 2 ** 20),
-        )(by_head(query_in), by_head(attn_out), by_head(grad_out), log_sum.transpose(2, 1, 0),
-          key_cache.transpose(1, 0, 2), value_cache.transpose(1, 0, 2))
+            scratch_shapes=[pltpu.SemaphoreType.DMA((3,))],
+            compiler_params=pltpu.CompilerParams(vmem_limit_bytes=2 ** 20),
+        )(*(pltpu.with_memory_space_constraint(x, pltpu.VMEM) for x in (grad_q, grad_k, grad_v)))
         grad_q = grad_q.reshape(n_slices, q_heads, rows8, head_dim).transpose(0, 2, 1, 3)
         return grad_q, grad_k.reshape(key_rows, kv_heads, head_dim), grad_v.reshape(key_rows, kv_heads, head_dim)
 

time: 91.3 us -> 82.7 us (0.906)
  local copies, waits for them, and re-layouts: 10.8 us -> 0 us
  Pallas kernels: 79.6 us -> 81.9 us
    unnamed x5 -> x0, local copies, waits for them, and re-layouts: 7.49 us -> none
    transpose x1 -> x0, local copies, waits for them, and re-layouts: 3.33 us -> none  [local_backward(): value_cache.transpose(1, 0, 2)]
    pallas_call x0 -> x1, Pallas kernels: none -> 2.46 us  [local_backward(): pl.pallas_call(store_results, out_shape=tuple((jax.ShapeDtypeStruct(x.sha...]
where the time goes in v2:
time: 82.7 us; the launch traced here: 82.6 us
  Pallas kernels  81.9 us (99%)
    pallas_call x1, Pallas kernels, local_backward(): pl.pallas_call(kernel, out_shape=(jax.ShapeDtypeStruct((n_slices, kv_head...  79.5 us
    pallas_call x1, Pallas kernels, local_backward(): pl.pallas_call(store_results, out_shape=tuple((jax.ShapeDtypeStruct(x.sha...  2.46 us

profile of v2, /device:TPU:0, one launch (start us, length us, event | category | flops | bytes accessed | tf_op | source)
XLA Modules:
  0.0 82.6 jit_solution(12039209440977120942)
XLA Ops:
  0.6 79.5 %shard_map.85 = (bf16[32,2,48,128]{3,2,1,0:T(8,128)(2,1)S(1)}, f32[4608,128]{1,0:T(8,128)S(1)}, f32[4608,128]{1,0:T(8,128)S(1)}) custom-call(bf16[32,2,48,128]{3,2,1,0:T(8,128)(2,1)} %bitcast.19, bf16[32,2,48,128]{3,2,1,0:T(8,128)(2,1)} %bitcast.20, bf16[32,2,48,128]{3,2,1,0:T(8,128)(2,1)} %bitcast.21, f32[12,8,32]{2,1,0:T(8,128)} %bitcast.22, ...), custom_call_target="tpu_custom_call" | custom-call | tf_op jit(solution)/shard_map/pallas_call | solution.py:305
  80.1 2.5 %shard_map.86 = (bf16[32,2,48,128]{3,2,1,0:T(8,128)(2,1)}, f32[4608,128]{1,0:T(8,128)}, f32[4608,128]{1,0:T(8,128)}) custom-call(bf16[32,2,48,128]{3,2,1,0:T(8,128)(2,1)S(1)} %get-tuple-element.9.dq_in, f32[4608,128]{1,0:T(8,128)S(1)} %get-tuple-element.10.dk_in, f32[4608,128]{1,0:T(8,128)S(1)} %get-tuple-element.11.dv_in), custom_call_target="tpu_custom_call" | custom-call | tf_op jit(solution)/shard_map/pallas_call | solution.py:319

commit v3 on v2

--- a/solution.py
+++ b/solution.py
@@ -1,3 +1,5 @@
+import functools
+
 import jax
 import jax.numpy as jnp
 from jax import lax
@@ -11,8 +13,8 @@
 NN = (((1,), (0,)), ((), ()))
 KEY_BLOCK = 256
 OWN, PEER, ACROSS, DIAG = 0, 1, 2, 3
-STEPS = [(0, 0), (1, 0), (0, 1), (2, 0), (3, 0), (1, 1), (2, 1), (3, 1), (0, 2), (2, 2), (3, 2), (1, 2), (2, 3), (3, 3), (0, 3), (1, 3)]
-REDUCE_AT = [5, 8, 11, 14]
+STEPS = [(0, 0), (1, 0), (0, 1), (2, 0), (3, 0), (2, 1), (3, 1), (1, 1), (2, 2), (3, 2), (2, 3), (3, 3), (0, 2), (1, 2), (0, 3), (1, 3)]
+REDUCE_AT = [5, 7, 10, 12]
 
 
 def dot(a, b, dims=NN):
@@ -35,7 +37,8 @@
     n_blocks = key_rows // KEY_BLOCK
     scale = head_dim ** -0.5
     exp_scale = scale * LOG2E
-    first_masked = max(0, prefix - (cp_size - 1) * key_rows) // KEY_BLOCK
+    last = cp_size - 1
+    assert last * key_rows <= prefix
 
     def kernel(q_hbm, o_hbm, g_hbm, l_hbm, k_hbm, v_hbm, dq_out, dk_out, dv_out,
                q_all, g_all, stat_all, o_own, lse_own, k_raw, v_raw, k_all, v_all, dk_t, dv_t, dq_all,
@@ -129,7 +132,7 @@
                 for kv in range(2):
                     split[kv, pl.ds(block * KEY_BLOCK, KEY_BLOCK)] = wide[pl.ds(2 * block * KEY_BLOCK + kv, KEY_BLOCK, stride=2)].astype(jnp.bfloat16)
 
-        def step_body(step, carry):
+        def step_body(on_last, step, carry):
             slot = table(step, [a for a, _ in STEPS])
             ch = table(step, [b for _, b in STEPS])
             kv, half = ch // 2, ch % 2
@@ -163,12 +166,12 @@
                     lse_rep[at] = jnp.broadcast_to(st[:, s:s + 1], (rows8, 128))
                     del_rep[at] = jnp.broadcast_to(st[:, n_slices + s:n_slices + s + 1], (rows8, 128))
 
-            def scores(block, p_buf, s_buf):
+            def scores(block, p_buf, s_buf, masked):
                 keys = pl.ds(block * KEY_BLOCK, KEY_BLOCK)
                 logits = dot(q_all[slot, ch].reshape(rows, head_dim), k_all[kv, keys], NT)
                 lse = lse_rep[...]
                 prob = jnp.exp2(logits * exp_scale - jnp.concatenate([lse, lse], 1))
-                if block >= first_masked:
+                if masked:
                     first = me * key_rows + block * KEY_BLOCK - prefix - half * (half_slices * slice_len) - source * rows8
                     key_pos = lax.broadcasted_iota(jnp.int32, (rows, KEY_BLOCK), 1) + first
                     pos = row_pos[...]
@@ -189,10 +192,12 @@
                     dq_all[slot, ch] += part_q
 
             bufs = ((p_a, s_a), (p_b, s_b))
-            scores(0, *bufs[0])
+
+            masked = [on_last and last * key_rows + (block + 1) * KEY_BLOCK > prefix for block in range(n_blocks)]
+            scores(0, *bufs[0], masked[0])
             for block in range(n_blocks):
                 if block + 1 < n_blocks:
-                    scores(block + 1, *bufs[(block + 1) % 2])
+                    scores(block + 1, *bufs[(block + 1) % 2], masked[block + 1])
                 grads(block, *bufs[block % 2])
 
             @pl.when(slot == PEER)
@@ -213,7 +218,10 @@
 
             return carry
 
-        lax.fori_loop(0, len(STEPS), step_body, 0)
+        for on_last in (False, True):
+            @pl.when((me == last) == on_last)
+            def _(on_last=on_last):
+                lax.fori_loop(0, len(STEPS), functools.partial(step_body, on_last), 0)
 
         for acc_t, out, factor in ((dv_t, dv_out, None), (dk_t, dk_out, scale)):
             for block in range(n_blocks):

time: 82.7 us -> 77.4 us (0.936)
  Pallas kernels: 81.9 us -> 76.6 us
    pallas_call x1, Pallas kernels: 79.5 us -> 74.2 us  [local_backward(): pl.pallas_call(kernel, out_shape=(jax.ShapeDtypeStruct((n_slices, kv_head...]
where the time goes in v3:
time: 77.4 us; the launch traced here: 77.3 us
  Pallas kernels  76.6 us (99%)
    pallas_call x1, Pallas kernels, local_backward(): pl.pallas_call(kernel, out_shape=(jax.ShapeDtypeStruct((n_slices, kv_head...  74.2 us
    pallas_call x1, Pallas kernels, local_backward(): pl.pallas_call(store_results, out_shape=tuple((jax.ShapeDtypeStruct(x.sha...  2.46 us

profile of v3, /device:TPU:0, one launch (start us, length us, event | category | flops | bytes accessed | tf_op | source)
XLA Modules:
  0.0 77.3 jit_solution(1139372567535654852)
XLA Ops:
  0.6 74.2 %shard_map.85 = (bf16[32,2,48,128]{3,2,1,0:T(8,128)(2,1)S(1)}, f32[4608,128]{1,0:T(8,128)S(1)}, f32[4608,128]{1,0:T(8,128)S(1)}) custom-call(bf16[32,2,48,128]{3,2,1,0:T(8,128)(2,1)} %bitcast.19, bf16[32,2,48,128]{3,2,1,0:T(8,128)(2,1)} %bitcast.20, bf16[32,2,48,128]{3,2,1,0:T(8,128)(2,1)} %bitcast.21, f32[12,8,32]{2,1,0:T(8,128)} %bitcast.22, ...), custom_call_target="tpu_custom_call" | custom-call | tf_op jit(solution)/shard_map/pallas_call | solution.py:313
  74.8 2.5 %shard_map.86 = (bf16[32,2,48,128]{3,2,1,0:T(8,128)(2,1)}, f32[4608,128]{1,0:T(8,128)}, f32[4608,128]{1,0:T(8,128)}) custom-call(bf16[32,2,48,128]{3,2,1,0:T(8,128)(2,1)S(1)} %get-tuple-element.9.dq_in, f32[4608,128]{1,0:T(8,128)S(1)} %get-tuple-element.10.dk_in, f32[4608,128]{1,0:T(8,128)S(1)} %get-tuple-element.11.dv_in), custom_call_target="tpu_custom_call" | custom-call | tf_op jit(solution)/shard_map/pallas_call | solution.py:327

commit v4 on v3

--- a/solution.py
+++ b/solution.py
@@ -41,7 +41,7 @@
     assert last * key_rows <= prefix
 
     def kernel(q_hbm, o_hbm, g_hbm, l_hbm, k_hbm, v_hbm, dq_out, dk_out, dv_out,
-               q_all, g_all, stat_all, o_own, lse_own, k_raw, v_raw, k_all, v_all, dk_t, dv_t, dq_all,
+               q_all, g_all, stat_all, stat_pack, o_own, lse_own, lse_wide, k_raw, v_raw, k_all, v_all, dk_t, dv_t, dq_all,
                from_peer_own, from_peer_across, from_across, q_t, g_t, p_a, s_a, p_b, s_b,
                lse_rep, del_rep, row_pos,
                load_sem, q_recv, g_recv, stat_recv, q_send, g_send, stat_send,
@@ -78,7 +78,7 @@
             return q, g
 
         def send_stat(src_slot, dst_slot, other):
-            return pltpu.make_async_remote_copy(stat_all.at[src_slot], stat_all.at[dst_slot], stat_send.at[dst_slot], stat_recv.at[dst_slot], device_id={'cp': other}, device_id_type=MESH)
+            return pltpu.make_async_remote_copy(stat_pack.at[src_slot], stat_pack.at[dst_slot], stat_send.at[dst_slot], stat_recv.at[dst_slot], device_id={'cp': other}, device_id_type=MESH)
 
         def forward_rows(ch):
             q = pltpu.make_async_remote_copy(q_all.at[ACROSS, ch], q_all.at[DIAG, ch], q_send.at[DIAG, ch], q_recv.at[DIAG, ch], device_id={'cp': peer}, device_id_type=MESH)
@@ -94,29 +94,43 @@
         def send_reduced(ch):
             return pltpu.make_async_remote_copy(dq_all.at[ACROSS, ch], from_across.at[ch], part_send.at[2, ch], part_recv.at[2, ch], device_id={'cp': across}, device_id_type=MESH)
 
+        def unpack_stats(slot):
+            both = stat_pack[slot].reshape(unit, 128)
+            stat_all[slot, pl.ds(0, group)] = both.reshape(group, rows8, 128)
+            stat_all[slot, pl.ds(group, group)] = pltpu.roll(both, 128 - 2 * n_slices, 1).reshape(group, rows8, 128)
+
         pl.semaphore_wait(barrier, 2)
-        for slot, other in ((ACROSS, across), (PEER, peer)):
-            for copy in send_rows(0, slot, other):
+
+        def start_rows(ch, slot, other):
+            for copy in send_rows(ch, slot, other):
                 copy.start()
+
+        pl.when(core == 0)(lambda: start_rows(0, ACROSS, across))
+        start_rows(0, PEER, peer)
 
         for copy in loads[:9]:
             copy.wait()
         lane = lax.broadcasted_iota(jnp.int32, (unit, 128), 1)
+        lse_wide[...] = jnp.zeros_like(lse_wide)
+        lse_wide[:, :, pl.ds(0, n_slices)] = lse_own[...] * LOG2E
+        stats = []
         for kv in range(2):
             acc = jnp.zeros((unit, 128), jnp.float32)
             for s in range(n_slices):
                 ch = kv * 2 + s // half_slices
                 prod = g_all[OWN, ch, s % half_slices].astype(jnp.float32) * o_own[ch, s % half_slices].astype(jnp.float32)
-                acc = jnp.where(lane == n_slices + s, jnp.sum(prod, axis=1, keepdims=True), acc)
-            stat_all[OWN, pl.ds(kv * group, group)] = acc.reshape(group, rows8, 128)
-        stat_all[OWN, :, :, pl.ds(0, n_slices)] = lse_own[...] * LOG2E
+                acc = jnp.where(lane == 2 * n_slices * kv + n_slices + s, jnp.sum(prod, axis=1, keepdims=True), acc)
+            lse = lse_wide[pl.ds(kv * group, group)].reshape(unit, 128)
+            stats.append(jnp.where(lane % (2 * n_slices) < n_slices, pltpu.roll(lse, 2 * n_slices, 1) if kv else lse, acc))
+        stat_pack[OWN] = jnp.where(lane < 2 * n_slices, stats[0], stats[1]).reshape(group, rows8, 128)
+        pl.when(core == 1)(lambda: start_rows(0, ACROSS, across))
         for slot, other in ((ACROSS, across), (PEER, peer)):
             send_stat(OWN, slot, other).start()
         for ch in range(1, 4):
             for slot, other in ((ACROSS, across), (PEER, peer)):
-                for copy in send_rows(ch, slot, other):
-                    copy.start()
-
+                start_rows(ch, slot, other)
+
+        unpack_stats(OWN)
         dk_t[...] = jnp.zeros_like(dk_t)
         dv_t[...] = jnp.zeros_like(dv_t)
         token = lax.broadcasted_iota(jnp.int32, (rows8, 128), 0)
@@ -145,7 +159,8 @@
 
             @pl.when(jnp.logical_and(slot != OWN, ch == 0))
             def _():
-                pltpu.make_async_remote_copy(stat_all.at[slot], stat_all.at[slot], stat_send.at[slot], stat_recv.at[slot], device_id={'cp': peer}, device_id_type=MESH).wait_recv()
+                pltpu.make_async_remote_copy(stat_pack.at[slot], stat_pack.at[slot], stat_send.at[slot], stat_recv.at[slot], device_id={'cp': peer}, device_id_type=MESH).wait_recv()
+                unpack_stats(slot)
 
             @pl.when(slot == ACROSS)
             def _():
@@ -252,8 +267,10 @@
         pltpu.VMEM((4, 4) + chunk, bf16),
         pltpu.VMEM((4, 4) + chunk, bf16),
         pltpu.VMEM((4, 2 * group, rows8, 128), f32),
+        pltpu.VMEM((4, group, rows8, 128), f32),
         pltpu.VMEM((4,) + chunk, bf16),
         pltpu.VMEM((2 * group, rows8, n_slices), f32),
+        pltpu.VMEM((2 * group, rows8, 128), f32),
         pltpu.VMEM((2 * key_rows, head_dim), bf16),
         pltpu.VMEM((2 * key_rows, head_dim), bf16),
         pltpu.VMEM((2, key_rows, head_dim), bf16),

time: 77.4 us -> 76.2 us (0.984)
  Pallas kernels: 76.6 us -> 75.3 us
    pallas_call x1, Pallas kernels: 74.2 us -> 72.8 us  [local_backward(): pl.pallas_call(kernel, out_shape=(jax.ShapeDtypeStruct((n_slices, kv_head...]
where the time goes in v4:
time: 76.2 us; the launch traced here: 75.9 us
  Pallas kernels  75.3 us (99%)
    pallas_call x1, Pallas kernels, local_backward(): pl.pallas_call(kernel, out_shape=(jax.ShapeDtypeStruct((n_slices, kv_head...  72.8 us
    pallas_call x1, Pallas kernels, local_backward(): pl.pallas_call(store_results, out_shape=tuple((jax.ShapeDtypeStruct(x.sha...  2.46 us

profile of v4, /device:TPU:0, one launch (start us, length us, event | category | flops | bytes accessed | tf_op | source)
XLA Modules:
  0.0 75.9 jit_solution(3155567867897972062)
XLA Ops:
  0.6 72.8 %shard_map.85 = (bf16[32,2,48,128]{3,2,1,0:T(8,128)(2,1)S(1)}, f32[4608,128]{1,0:T(8,128)S(1)}, f32[4608,128]{1,0:T(8,128)S(1)}) custom-call(bf16[32,2,48,128]{3,2,1,0:T(8,128)(2,1)} %bitcast.19, bf16[32,2,48,128]{3,2,1,0:T(8,128)(2,1)} %bitcast.20, bf16[32,2,48,128]{3,2,1,0:T(8,128)(2,1)} %bitcast.21, f32[12,8,32]{2,1,0:T(8,128)} %bitcast.22, ...), custom_call_target="tpu_custom_call" | custom-call | tf_op jit(solution)/shard_map/pallas_call | solution.py:330
  73.4 2.5 %shard_map.86 = (bf16[32,2,48,128]{3,2,1,0:T(8,128)(2,1)}, f32[4608,128]{1,0:T(8,128)}, f32[4608,128]{1,0:T(8,128)}) custom-call(bf16[32,2,48,128]{3,2,1,0:T(8,128)(2,1)S(1)} %get-tuple-element.9.dq_in, f32[4608,128]{1,0:T(8,128)S(1)} %get-tuple-element.10.dk_in, f32[4608,128]{1,0:T(8,128)S(1)} %get-tuple-element.11.dv_in), custom_call_target="tpu_custom_call" | custom-call | tf_op jit(solution)/shard_map/pallas_call | solution.py:344

commit v5 on v4

--- a/solution.py
+++ b/solution.py
@@ -15,6 +15,7 @@
 OWN, PEER, ACROSS, DIAG = 0, 1, 2, 3
 STEPS = [(0, 0), (1, 0), (0, 1), (2, 0), (3, 0), (2, 1), (3, 1), (1, 1), (2, 2), (3, 2), (2, 3), (3, 3), (0, 2), (1, 2), (0, 3), (1, 3)]
 REDUCE_AT = [5, 7, 10, 12]
+REDUCE_NEAR = [5, 7, 10, 14]
 
 
 def dot(a, b, dims=NN):
@@ -105,7 +106,7 @@
             for copy in send_rows(ch, slot, other):
                 copy.start()
 
-        pl.when(core == 0)(lambda: start_rows(0, ACROSS, across))
+        start_rows(0, ACROSS, across)
         start_rows(0, PEER, peer)
 
         for copy in loads[:9]:
@@ -123,7 +124,6 @@
             lse = lse_wide[pl.ds(kv * group, group)].reshape(unit, 128)
             stats.append(jnp.where(lane % (2 * n_slices) < n_slices, pltpu.roll(lse, 2 * n_slices, 1) if kv else lse, acc))
         stat_pack[OWN] = jnp.where(lane < 2 * n_slices, stats[0], stats[1]).reshape(group, rows8, 128)
-        pl.when(core == 1)(lambda: start_rows(0, ACROSS, across))
         for slot, other in ((ACROSS, across), (PEER, peer)):
             send_stat(OWN, slot, other).start()
         for ch in range(1, 4):
@@ -223,7 +223,10 @@
             def _():
                 send_diag_part(ch).start()
 
-            reduce_ch = table(step, [REDUCE_AT.index(i) if i in REDUCE_AT else -1 for i in range(len(STEPS))])
+            reduce_ch = jnp.where(
+                core == 1,
+                table(step, [REDUCE_NEAR.index(i) if i in REDUCE_NEAR else -1 for i in range(len(STEPS))]),
+                table(step, [REDUCE_AT.index(i) if i in REDUCE_AT else -1 for i in range(len(STEPS))]))
 
             @pl.when(reduce_ch >= 0)
             def _():

time: 76.2 us -> 76 us (level)
  the two profiles are of different devices: /device:TPU:0 before, /device:TPU:1 now
where the time goes in v5:
time: 76 us; the launch traced here: 75.8 us
  Pallas kernels  75.2 us (99%)
    pallas_call x1, Pallas kernels, local_backward(): pl.pallas_call(kernel, out_shape=(jax.ShapeDtypeStruct((n_slices, kv_head...  72.7 us
    pallas_call x1, Pallas kernels, local_backward(): pl.pallas_call(store_results, out_shape=tuple((jax.ShapeDtypeStruct(x.sha...  2.46 us

profile of v5, /device:TPU:1, one launch (start us, length us, event | category | flops | bytes accessed | tf_op | source)
XLA Modules:
  0.0 75.8 jit_solution(14574282922010287046)
XLA Ops:
  0.6 72.7 %shard_map.85 = (bf16[32,2,48,128]{3,2,1,0:T(8,128)(2,1)S(1)}, f32[4608,128]{1,0:T(8,128)S(1)}, f32[4608,128]{1,0:T(8,128)S(1)}) custom-call(bf16[32,2,48,128]{3,2,1,0:T(8,128)(2,1)} %bitcast.19, bf16[32,2,48,128]{3,2,1,0:T(8,128)(2,1)} %bitcast.20, bf16[32,2,48,128]{3,2,1,0:T(8,128)(2,1)} %bitcast.21, f32[12,8,32]{2,1,0:T(8,128)} %bitcast.22, ...), custom_call_target="tpu_custom_call" | custom-call | tf_op jit(solution)/shard_map/pallas_call | solution.py:333
  73.4 2.5 %shard_map.86 = (bf16[32,2,48,128]{3,2,1,0:T(8,128)(2,1)}, f32[4608,128]{1,0:T(8,128)}, f32[4608,128]{1,0:T(8,128)}) custom-call(bf16[32,2,48,128]{3,2,1,0:T(8,128)(2,1)S(1)} %get-tuple-element.9.dq_in, f32[4608,128]{1,0:T(8,128)S(1)} %get-tuple-element.10.dk_in, f32[4608,128]{1,0:T(8,128)S(1)} %get-tuple-element.11.dv_in), custom_call_target="tpu_custom_call" | custom-call | tf_op jit(solution)/shard_map/pallas_call | solution.py:347

commit v6 on v5

--- a/solution.py
+++ b/solution.py
@@ -15,7 +15,7 @@
 OWN, PEER, ACROSS, DIAG = 0, 1, 2, 3
 STEPS = [(0, 0), (1, 0), (0, 1), (2, 0), (3, 0), (2, 1), (3, 1), (1, 1), (2, 2), (3, 2), (2, 3), (3, 3), (0, 2), (1, 2), (0, 3), (1, 3)]
 REDUCE_AT = [5, 7, 10, 12]
-REDUCE_NEAR = [5, 7, 10, 14]
+REDUCE_NEAR = [5, 7, 12, 13]
 
 
 def dot(a, b, dims=NN):

time: 76 us -> 76 us (level)
  no operation moved by 1% of the time
where the time goes in v6:
time: 76 us; the launch traced here: 75.8 us
  Pallas kernels  75.2 us (99%)
    pallas_call x1, Pallas kernels, local_backward(): pl.pallas_call(kernel, out_shape=(jax.ShapeDtypeStruct((n_slices, kv_head...  72.7 us
    pallas_call x1, Pallas kernels, local_backward(): pl.pallas_call(store_results, out_shape=tuple((jax.ShapeDtypeStruct(x.sha...  2.46 us

profile of v6, /device:TPU:1, one launch (start us, length us, event | category | flops | bytes accessed | tf_op | source)
XLA Modules:
  0.0 75.8 jit_solution(9374126846658382787)
XLA Ops:
  0.6 72.7 %shard_map.85 = (bf16[32,2,48,128]{3,2,1,0:T(8,128)(2,1)S(1)}, f32[4608,128]{1,0:T(8,128)S(1)}, f32[4608,128]{1,0:T(8,128)S(1)}) custom-call(bf16[32,2,48,128]{3,2,1,0:T(8,128)(2,1)} %bitcast.19, bf16[32,2,48,128]{3,2,1,0:T(8,128)(2,1)} %bitcast.20, bf16[32,2,48,128]{3,2,1,0:T(8,128)(2,1)} %bitcast.21, f32[12,8,32]{2,1,0:T(8,128)} %bitcast.22, ...), custom_call_target="tpu_custom_call" | custom-call | tf_op jit(solution)/shard_map/pallas_call | solution.py:333
  73.4 2.5 %shard_map.86 = (bf16[32,2,48,128]{3,2,1,0:T(8,128)(2,1)}, f32[4608,128]{1,0:T(8,128)}, f32[4608,128]{1,0:T(8,128)}) custom-call(bf16[32,2,48,128]{3,2,1,0:T(8,128)(2,1)S(1)} %get-tuple-element.9.dq_in, f32[4608,128]{1,0:T(8,128)S(1)} %get-tuple-element.10.dk_in, f32[4608,128]{1,0:T(8,128)S(1)} %get-tuple-element.11.dv_in), custom_call_target="tpu_custom_call" | custom-call | tf_op jit(solution)/shard_map/pallas_call | solution.py:347
